TPU v7x, 32 devices: a whole 2x2x4 slice. The times are simulated.
32 devices in a mesh: dp: 8 (over z, y), section: 4 (over x, core).
Axes of the slice: x: 2, y: 2, z: 4, core: 2. Of those that a mesh axis runs over, the one named last changes fastest.
Arguments:
- patches: bfloat16 [64, 197, 1024], P('dp'), may hold values from -6 to 6
- ln1_gain: float32 [4, 1024], P('section'), may hold values from 0.5 to 1.5
- w_qkv: bfloat16 [4, 1024, 3072], P('section'), may hold values from -1 to 1
- w_out: bfloat16 [4, 1024, 1024], P('section'), may hold values from -0.1875 to 0.1875
- ln2_gain: float32 [4, 1024], P('section'), may hold values from 0.5 to 1.5
- w_fc1: bfloat16 [4, 1024, 2048], P('section'), may hold values from -0.1875 to 0.1875
- w_fc2: bfloat16 [4, 2048, 1024], P('section'), may hold values from -0.125 to 0.125
- final_norm_gain: float32 [1024], replicated, may hold values from 0.5 to 1.5
- w_head: bfloat16 [1024, 256], replicated, may hold values from -0.1875 to 0.1875
- online_embeddings: bfloat16 [64, 256], P('dp'), may hold values from -60 to 60
- queue: bfloat16 [32768, 256], P(('dp', 'section')), may hold values from -1 to 1, as said below
- owner: int32 [64], replicated, may hold values from 0 to 63, each once
- pointer: int32 [8], P('dp'), may hold values from 0 to 4088
Outputs:
- momentum_embeddings: bfloat16 [64, 256], P('dp')
- query_loss: float32 [64], P('dp')
- total_loss: float32 [], replicated
- new_queue: bfloat16 [32768, 256], P(('dp', 'section'))
Inputs may be any that keep to these rules, and one draw needn't show every extreme that they name: `queue`: every row has Euclidean norm below 1. Each value appears once: key j goes to group owner[j] // 8, so every group receives exactly 8 keys. `pointer`: first row of the group's shard where its new keys are written.
All inputs are finite; a program needn't handle non-finite values.
Results may differ from a plain program's by a relative error of at most 0.02.
Values may be sent and summed in bfloat16 or wider, within the bound.
No kernel may reach another device: no remote copies, remote signals or barrier semaphores. Data moves between devices by JAX's collectives and lax.ppermute only.
A program may use at most 128 MiB of HBM per device.

v0:
```python
import math
import jax
import jax.numpy as jnp
from jax import lax
from jax.sharding import PartitionSpec as P

HEADS = 16
HEAD_DIM = 64
TOKS = 197
IMG_MB = 2
contrastive_sharpness = 0.2


def from_behind(value, axis, steps):
    count = lax.axis_size(axis)
    initial, last = (max(0, -steps), min(count, count - steps))
    return lax.ppermute(value, axis, [(source, source + steps) for source in range(initial, last)])


def broadcast(value, axis, source):
    kept = jnp.where(lax.axis_index(axis) == source, value, 0).astype(value.dtype)
    return lax.psum(kept, axis)


def layer_norm(values, gain):
    center = values - jnp.mean(values, axis=-1, keepdims=True)
    spread = jnp.mean(center * center, axis=-1, keepdims=True)
    return center * lax.rsqrt(spread + 1e-06) * gain


def encoder_block(hidden, gain_one, qkv_weight, out_weight, gain_two, first_weight, second_weight):
    images = hidden.shape[0]
    width = hidden.shape[2]
    stream = hidden.astype(jnp.float32)
    normed = layer_norm(stream, gain_one).astype(jnp.bfloat16).reshape(images * TOKS, width)
    packed = jnp.dot(normed, qkv_weight, preferred_element_type=jnp.float32).astype(jnp.bfloat16)
    packed = packed.reshape(images, TOKS, 3, HEADS, HEAD_DIM)
    similarity_matrix = jnp.einsum(
        "bqhd,bkhd->bhqk", packed[:, :, 0], packed[:, :, 1], preferred_element_type=jnp.float32
    )
    similarity_matrix = similarity_matrix / math.sqrt(HEAD_DIM)
    peak = jnp.max(similarity_matrix, axis=-1, keepdims=True)
    expo = jnp.exp(similarity_matrix - peak)
    probs = (expo / jnp.sum(expo, axis=-1, keepdims=True)).astype(jnp.bfloat16)
    context = jnp.einsum(
        "bhqk,bkhd->bqhd", probs, packed[:, :, 2], preferred_element_type=jnp.float32
    )
    context = context.astype(jnp.bfloat16).reshape(images * TOKS, width)
    stream = stream + jnp.dot(context, out_weight, preferred_element_type=jnp.float32).reshape(
        images, TOKS, width
    )
    normed = layer_norm(stream, gain_two).astype(jnp.bfloat16).reshape(images * TOKS, width)
    inner = jax.nn.gelu(
        jnp.dot(normed, first_weight, preferred_element_type=jnp.float32), approximate=False
    )
    inner = inner.astype(jnp.bfloat16)
    stream = stream + jnp.dot(inner, second_weight, preferred_element_type=jnp.float32).reshape(
        images, TOKS, width
    )
    return stream.astype(jnp.bfloat16)


def key_head(class_rows, final_norm_gain, w_head):
    normed = layer_norm(class_rows.astype(jnp.float32), final_norm_gain).astype(jnp.bfloat16)
    projected = jnp.dot(normed, w_head, preferred_element_type=jnp.float32)
    scale = lax.rsqrt(1.0 + jnp.sum(projected * projected, axis=1, keepdims=True))
    return (projected * scale).astype(jnp.bfloat16)


def on_device(
    patches,
    ln1_gain,
    w_qkv,
    w_out,
    ln2_gain,
    w_fc1,
    w_fc2,
    final_norm_gain,
    w_head,
    online_embeddings,
    queue,
    owner,
    pointer,
):
    sections = lax.axis_size("section")
    section_index = lax.axis_index("section")
    group_index = lax.axis_index("dp")
    group_images = patches.shape[0]
    width = patches.shape[2]
    batch_size = IMG_MB // 2
    blocks = group_images // batch_size
    feeds = patches.reshape(blocks, batch_size, TOKS, width)

    def run_block(hidden):
        return encoder_block(
            hidden, ln1_gain[0], w_qkv[0], w_out[0], ln2_gain[0], w_fc1[0], w_fc2[0]
        )

    def keep_block(hidden):
        return hidden

    def advance(tick, carry):
        incoming, finished = carry
        fresh = lax.dynamic_index_in_dim(feeds, jnp.minimum(tick, blocks - 1), 0, keepdims=False)
        source = jnp.where(section_index == 0, fresh, incoming)
        active = jnp.logical_and(tick >= section_index, tick - section_index < blocks)
        result = lax.cond(active, run_block, keep_block, source)
        place = jnp.clip(tick - (sections - 1), 0, blocks - 1)
        stored = lax.dynamic_update_index_in_dim(finished, result[:, 0, :], place, 0)
        finished = jnp.where(tick >= sections - 1, stored, finished)
        passed = from_behind(result, "section", 1)
        return (passed, finished)

    start = (jnp.zeros_like(feeds[0]), jnp.zeros((blocks, batch_size, width), jnp.bfloat16))
    passed, finished = lax.fori_loop(0, blocks + sections - 1, advance, start)
    resident_embeddings = key_head(finished.reshape(group_images, width), final_norm_gain, w_head)
    momentum_embeddings = broadcast(resident_embeddings, "section", sections - 1)
    query_rows_full = lax.all_gather(online_embeddings, "dp", axis=0, tiled=True)
    share = queue.shape[0]
    similarity_matrix = (
        jnp.einsum("tw,fw->tf", query_rows_full, queue, preferred_element_type=jnp.float32)
        / contrastive_sharpness
    )
    local_peak = jnp.max(similarity_matrix, axis=1)
    top = lax.pmax(local_peak, ("dp", "section"))
    total = lax.psum(jnp.sum(jnp.exp(similarity_matrix - top[:, None]), axis=1), ("dp", "section"))
    negative_all = top + jnp.log(total)
    negative = lax.dynamic_slice_in_dim(negative_all, group_index * group_images, group_images, 0)
    matching_similarity = (
        jnp.sum(
            online_embeddings.astype(jnp.float32) * momentum_embeddings.astype(jnp.float32), axis=1
        )
        / contrastive_sharpness
    )
    larger = jnp.maximum(negative, matching_similarity)
    query_loss = (
        larger
        + jnp.log(jnp.exp(negative - larger) + jnp.exp(matching_similarity - larger))
        - matching_similarity
    )
    loss_sum = lax.psum(jnp.sum(query_loss), "dp")
    total_loss = loss_sum / (group_images * lax.axis_size("dp"))
    every_key = lax.all_gather(momentum_embeddings, "dp", axis=0, tiled=True)
    wanted = group_index * group_images + jnp.arange(group_images, dtype=jnp.int32)
    selector = (owner[None, :] == wanted[:, None]).astype(jnp.bfloat16)
    incoming_keys = jnp.dot(selector, every_key, preferred_element_type=jnp.float32).astype(
        jnp.bfloat16
    )
    row_place = section_index * share + jnp.arange(share, dtype=jnp.int32)
    slot_index = row_place - pointer[0]
    placing = (slot_index[:, None] == jnp.arange(group_images, dtype=jnp.int32)[None, :]).astype(
        jnp.bfloat16
    )
    written = jnp.dot(placing, incoming_keys, preferred_element_type=jnp.float32).astype(
        jnp.bfloat16
    )
    inside = jnp.logical_and(slot_index >= 0, slot_index < group_images)
    new_queue = jnp.where(inside[:, None], written, queue)
    return (momentum_embeddings, query_loss, total_loss, new_queue)


def solution(mesh):
    placed = (
        P("dp", None, None),
        P("section", None),
        P("section", None, None),
        P("section", None, None),
        P("section", None),
        P("section", None, None),
        P("section", None, None),
        P(),
        P(),
        P("dp", None),
        P(("dp", "section"), None),
        P(),
        P("dp"),
    )
    return jax.shard_map(
        on_device,
        mesh=mesh,
        in_specs=placed,
        out_specs=(P("dp", None), P("dp"), P(), P(("dp", "section"), None)),
        check_vma=False,
    )
```

profile of v0, /device:TPU:0, one launch (start us, length us, event | category | flops | bytes accessed | tf_op | source)
XLA Modules:
  0.0 522.6 jit_solution(10496831233054502232)
XLA Ops:
  6.2 320.3 %while.17 = (s32[]{:T(128)}, bf16[1,197,1024]{2,1,0:T(8,128)(2,1)S(1)}, bf16[8,1,1024]{2,1,0:T(2,128)(2,1)S(1)}, s32[]{:T(128)}, pred[]{:T(512)}, /*index=5*/bf1...) while((s32[]{:T(128)}, ...), condition=%wide.region_9.10_spmd, body=%wide.region_0.9_spmd.sunk | while | flops 3499673600 | bytes 49231128 | solution.py:115
  7.4 22.1 %conditional.2 = (bf16[1,197,1024]{2,1,0:T(8,128)(2,1)S(1)}) conditional(s32[]{:T(128)} %convert_element_type.128, bf16[1,197,1024]{2,1,0:T(8,128)(2,1)S(1)} %bitcast_select_fusion.2, (bf16[1,197,1024]{2,1,0:T(8,128)(2,1)S(1)}, f32[1,1024]{1,0:T(1,128)S(1)}, bf16[1,1024,3072]{2,1,0:T(8,128)(2,1)}, bf16[1,1024,1024]{2,1,0:T(8,128)(2,1)}, ...), branch_computations={%region_1.1_spmd, %region_2.8_spmd} | conditional | flops 3499470848 | bytes 46394252 | solution.py:107
  20.7 8.7 %fusion.40 = bf16[1,197,1024]{2,1,0:T(8,128)(2,1)S(1)} fusion(f32[1,197,1024]{2,1,0:T(8,128)S(1)} %get-tuple-element.344, bf16[1,2048,1024]{2,1,0:T(8,128)(2,1)} %get-tuple-element.295, bf16[1,1024,2048]{2,1,0:T(8,128)(2,1)} %get-tuple-element.294, f32[1024]{0:T(1024)S(1)} %bitcast.93, f32[197]{0:T(256)S(1)} %add_rsqrt_fusion, ...), kind=kOutput, calls=%fused_computation.40 | convolution fusion | flops 1679990784 | bytes 9604648 | tf_op jit(solution)/shard_map/while/body/eval_jaxpr/cond/branch_1_fun/dot_general | solution.py:57
  33.2 22.1 %conditional.2 = (bf16[1,197,1024]{2,1,0:T(8,128)(2,1)S(1)}) conditional(s32[]{:T(128)} %convert_element_type.128, bf16[1,197,1024]{2,1,0:T(8,128)(2,1)S(1)} %bitcast_select_fusion.2, (bf16[1,197,1024]{2,1,0:T(8,128)(2,1)S(1)}, f32[1,1024]{1,0:T(1,128)S(1)}, bf16[1,1024,3072]{2,1,0:T(8,128)(2,1)}, bf16[1,1024,1024]{2,1,0:T(8,128)(2,1)}, ...), branch_computations={%region_1.1_spmd, %region_2.8_spmd} | conditional | flops 3499470848 | bytes 46394252 | solution.py:107
  60.0 22.1 %conditional.2 = (bf16[1,197,1024]{2,1,0:T(8,128)(2,1)S(1)}) conditional(s32[]{:T(128)} %convert_element_type.128, bf16[1,197,1024]{2,1,0:T(8,128)(2,1)S(1)} %bitcast_select_fusion.2, (bf16[1,197,1024]{2,1,0:T(8,128)(2,1)S(1)}, f32[1,1024]{1,0:T(1,128)S(1)}, bf16[1,1024,3072]{2,1,0:T(8,128)(2,1)}, bf16[1,1024,1024]{2,1,0:T(8,128)(2,1)}, ...), branch_computations={%region_1.1_spmd, %region_2.8_spmd} | conditional | flops 3499470848 | bytes 46394252 | solution.py:107
  73.4 8.7 %fusion.40 = bf16[1,197,1024]{2,1,0:T(8,128)(2,1)S(1)} fusion(f32[1,197,1024]{2,1,0:T(8,128)S(1)} %get-tuple-element.344, bf16[1,2048,1024]{2,1,0:T(8,128)(2,1)} %get-tuple-element.295, bf16[1,1024,2048]{2,1,0:T(8,128)(2,1)} %get-tuple-element.294, f32[1024]{0:T(1024)S(1)} %bitcast.93, f32[197]{0:T(256)S(1)} %add_rsqrt_fusion, ...), kind=kOutput, calls=%fused_computation.40 | convolution fusion | flops 1679990784 | bytes 9604648 | tf_op jit(solution)/shard_map/while/body/eval_jaxpr/cond/branch_1_fun/dot_general | solution.py:57
  90.0 22.1 %conditional.2 = (bf16[1,197,1024]{2,1,0:T(8,128)(2,1)S(1)}) conditional(s32[]{:T(128)} %convert_element_type.128, bf16[1,197,1024]{2,1,0:T(8,128)(2,1)S(1)} %bitcast_select_fusion.2, (bf16[1,197,1024]{2,1,0:T(8,128)(2,1)S(1)}, f32[1,1024]{1,0:T(1,128)S(1)}, bf16[1,1024,3072]{2,1,0:T(8,128)(2,1)}, bf16[1,1024,1024]{2,1,0:T(8,128)(2,1)}, ...), branch_computations={%region_1.1_spmd, %region_2.8_spmd} | conditional | flops 3499470848 | bytes 46394252 | solution.py:107
  103.4 8.7 %fusion.40 = bf16[1,197,1024]{2,1,0:T(8,128)(2,1)S(1)} fusion(f32[1,197,1024]{2,1,0:T(8,128)S(1)} %get-tuple-element.344, bf16[1,2048,1024]{2,1,0:T(8,128)(2,1)} %get-tuple-element.295, bf16[1,1024,2048]{2,1,0:T(8,128)(2,1)} %get-tuple-element.294, f32[1024]{0:T(1024)S(1)} %bitcast.93, f32[197]{0:T(256)S(1)} %add_rsqrt_fusion, ...), kind=kOutput, calls=%fused_computation.40 | convolution fusion | flops 1679990784 | bytes 9604648 | tf_op jit(solution)/shard_map/while/body/eval_jaxpr/cond/branch_1_fun/dot_general | solution.py:57
  122.5 22.1 %conditional.2 = (bf16[1,197,1024]{2,1,0:T(8,128)(2,1)S(1)}) conditional(s32[]{:T(128)} %convert_element_type.128, bf16[1,197,1024]{2,1,0:T(8,128)(2,1)S(1)} %bitcast_select_fusion.2, (bf16[1,197,1024]{2,1,0:T(8,128)(2,1)S(1)}, f32[1,1024]{1,0:T(1,128)S(1)}, bf16[1,1024,3072]{2,1,0:T(8,128)(2,1)}, bf16[1,1024,1024]{2,1,0:T(8,128)(2,1)}, ...), branch_computations={%region_1.1_spmd, %region_2.8_spmd} | conditional | flops 3499470848 | bytes 46394252 | solution.py:107
  135.9 8.7 %fusion.40 = bf16[1,197,1024]{2,1,0:T(8,128)(2,1)S(1)} fusion(f32[1,197,1024]{2,1,0:T(8,128)S(1)} %get-tuple-element.344, bf16[1,2048,1024]{2,1,0:T(8,128)(2,1)} %get-tuple-element.295, bf16[1,1024,2048]{2,1,0:T(8,128)(2,1)} %get-tuple-element.294, f32[1024]{0:T(1024)S(1)} %bitcast.93, f32[197]{0:T(256)S(1)} %add_rsqrt_fusion, ...), kind=kOutput, calls=%fused_computation.40 | convolution fusion | flops 1679990784 | bytes 9604648 | tf_op jit(solution)/shard_map/while/body/eval_jaxpr/cond/branch_1_fun/dot_general | solution.py:57
  154.9 22.1 %conditional.2 = (bf16[1,197,1024]{2,1,0:T(8,128)(2,1)S(1)}) conditional(s32[]{:T(128)} %convert_element_type.128, bf16[1,197,1024]{2,1,0:T(8,128)(2,1)S(1)} %bitcast_select_fusion.2, (bf16[1,197,1024]{2,1,0:T(8,128)(2,1)S(1)}, f32[1,1024]{1,0:T(1,128)S(1)}, bf16[1,1024,3072]{2,1,0:T(8,128)(2,1)}, bf16[1,1024,1024]{2,1,0:T(8,128)(2,1)}, ...), branch_computations={%region_1.1_spmd, %region_2.8_spmd} | conditional | flops 3499470848 | bytes 46394252 | solution.py:107
  168.3 8.7 %fusion.40 = bf16[1,197,1024]{2,1,0:T(8,128)(2,1)S(1)} fusion(f32[1,197,1024]{2,1,0:T(8,128)S(1)} %get-tuple-element.344, bf16[1,2048,1024]{2,1,0:T(8,128)(2,1)} %get-tuple-element.295, bf16[1,1024,2048]{2,1,0:T(8,128)(2,1)} %get-tuple-element.294, f32[1024]{0:T(1024)S(1)} %bitcast.93, f32[197]{0:T(256)S(1)} %add_rsqrt_fusion, ...), kind=kOutput, calls=%fused_computation.40 | convolution fusion | flops 1679990784 | bytes 9604648 | tf_op jit(solution)/shard_map/while/body/eval_jaxpr/cond/branch_1_fun/dot_general | solution.py:57
  187.4 22.1 %conditional.2 = (bf16[1,197,1024]{2,1,0:T(8,128)(2,1)S(1)}) conditional(s32[]{:T(128)} %convert_element_type.128, bf16[1,197,1024]{2,1,0:T(8,128)(2,1)S(1)} %bitcast_select_fusion.2, (bf16[1,197,1024]{2,1,0:T(8,128)(2,1)S(1)}, f32[1,1024]{1,0:T(1,128)S(1)}, bf16[1,1024,3072]{2,1,0:T(8,128)(2,1)}, bf16[1,1024,1024]{2,1,0:T(8,128)(2,1)}, ...), branch_computations={%region_1.1_spmd, %region_2.8_spmd} | conditional | flops 3499470848 | bytes 46394252 | solution.py:107
  200.8 8.7 %fusion.40 = bf16[1,197,1024]{2,1,0:T(8,128)(2,1)S(1)} fusion(f32[1,197,1024]{2,1,0:T(8,128)S(1)} %get-tuple-element.344, bf16[1,2048,1024]{2,1,0:T(8,128)(2,1)} %get-tuple-element.295, bf16[1,1024,2048]{2,1,0:T(8,128)(2,1)} %get-tuple-element.294, f32[1024]{0:T(1024)S(1)} %bitcast.93, f32[197]{0:T(256)S(1)} %add_rsqrt_fusion, ...), kind=kOutput, calls=%fused_computation.40 | convolution fusion | flops 1679990784 | bytes 9604648 | tf_op jit(solution)/shard_map/while/body/eval_jaxpr/cond/branch_1_fun/dot_general | solution.py:57
  219.8 22.1 %conditional.2 = (bf16[1,197,1024]{2,1,0:T(8,128)(2,1)S(1)}) conditional(s32[]{:T(128)} %convert_element_type.128, bf16[1,197,1024]{2,1,0:T(8,128)(2,1)S(1)} %bitcast_select_fusion.2, (bf16[1,197,1024]{2,1,0:T(8,128)(2,1)S(1)}, f32[1,1024]{1,0:T(1,128)S(1)}, bf16[1,1024,3072]{2,1,0:T(8,128)(2,1)}, bf16[1,1024,1024]{2,1,0:T(8,128)(2,1)}, ...), branch_computations={%region_1.1_spmd, %region_2.8_spmd} | conditional | flops 3499470848 | bytes 46394252 | solution.py:107
  233.2 8.7 %fusion.40 = bf16[1,197,1024]{2,1,0:T(8,128)(2,1)S(1)} fusion(f32[1,197,1024]{2,1,0:T(8,128)S(1)} %get-tuple-element.344, bf16[1,2048,1024]{2,1,0:T(8,128)(2,1)} %get-tuple-element.295, bf16[1,1024,2048]{2,1,0:T(8,128)(2,1)} %get-tuple-element.294, f32[1024]{0:T(1024)S(1)} %bitcast.93, f32[197]{0:T(256)S(1)} %add_rsqrt_fusion, ...), kind=kOutput, calls=%fused_computation.40 | convolution fusion | flops 1679990784 | bytes 9604648 | tf_op jit(solution)/shard_map/while/body/eval_jaxpr/cond/branch_1_fun/dot_general | solution.py:57
  252.3 30.1 %collective-permute-start = (bf16[1,197,1024]{2,1,0:T(8,128)(2,1)S(1)}, bf16[1,197,1024]{2,1,0:T(8,128)(2,1)S(1)}, u32[]{:S(2)}, u32[]{:S(2)}) collective-permute-start(bf16[1,197,1024]{2,1,0:T(8,128)(2,1)S(1)} %get-tuple-element.476), channel_id=1, source_target_pairs={{0,1},{1,2},{2,3},{4,5},{5,6},{6,7},{8,9},{9,10},{10,11},{12,13},{... | collective-permute-start | bytes 1210376 | tf_op jit(solution)/shard_map/while/body/eval_jaxpr/ppermute | solution.py:17
  295.1 30.1 %collective-permute-start = (bf16[1,197,1024]{2,1,0:T(8,128)(2,1)S(1)}, bf16[1,197,1024]{2,1,0:T(8,128)(2,1)S(1)}, u32[]{:S(2)}, u32[]{:S(2)}) collective-permute-start(bf16[1,197,1024]{2,1,0:T(8,128)(2,1)S(1)} %get-tuple-element.476), channel_id=1, source_target_pairs={{0,1},{1,2},{2,3},{4,5},{5,6},{6,7},{8,9},{9,10},{10,11},{12,13},{... | collective-permute-start | bytes 1210376 | tf_op jit(solution)/shard_map/while/body/eval_jaxpr/ppermute | solution.py:17
  327.3 24.5 %psum.21 = bf16[8,256]{1,0:T(8,128)(2,1)S(1)} all-reduce(bf16[8,256]{1,0:T(8,128)(2,1)S(1)} %fusion.136), channel_id=1, replica_groups=mesh['dp'=8,'section'=4] {'section'}, use_global_device_ids=true, to_apply=%region_13.14 | all-reduce | flops 2048 | bytes 8192 | tf_op jit(solution)/shard_map/psum | solution.py:22
  351.8 32.6 %all_gather.7 = bf16[64,256]{1,0:T(8,128)(2,1)S(1)} all-gather(bf16[8,256]{1,0:T(8,128)(2,1)S(1)} %psum.21), channel_id=1, replica_groups=mesh['dp'=8,'section'=4] {'dp'}, dimensions={0}, use_global_device_ids=true | all-gather | bytes 36864 | tf_op jit(solution)/shard_map/all_gather | solution.py:143
  386.5 30.6 %all_gather.6 = bf16[64,256]{1,0:T(8,128)(2,1)S(1)} all-gather(bf16[8,256]{1,0:T(8,128)(2,1)S(1)} %copy-done.4), channel_id=1, replica_groups=mesh['dp'=8,'section'=4] {'dp'}, dimensions={0}, use_global_device_ids=true | all-gather | bytes 36864 | tf_op jit(solution)/shard_map/all_gather | solution.py:118
  417.5 38.5 %pmax.7 = f32[64]{0:T(128)S(1)} all-reduce(f32[64]{0:T(128)S(1)} %get-tuple-element.347), channel_id=1, replica_groups=mesh['dp'=8,'section'=4] {'dp','section'}, use_global_device_ids=true, to_apply=%region_15.16 | all-reduce | flops 64 | bytes 512 | tf_op jit(solution)/shard_map/pmax | solution.py:125
  456.3 41.6 %psum.22 = f32[64]{0:T(128)S(1)} all-reduce(f32[64]{0:T(128)S(1)} %exponential_reduce_fusion), channel_id=1, replica_groups=mesh['dp'=8,'section'=4] {'dp','section'}, use_global_device_ids=true, to_apply=%region_17.18 | all-reduce | flops 64 | bytes 512 | tf_op jit(solution)/shard_map/psum | solution.py:126
  499.1 21.7 %psum.23 = f32[]{:T(128)} all-reduce(f32[]{:T(128)} %get-tuple-element.339), channel_id=1, replica_groups=mesh['dp'=8,'section'=4] {'dp'}, use_global_device_ids=true, to_apply=%region_20.21 | all-reduce | flops 1 | bytes 8 | tf_op jit(solution)/shard_map/psum | solution.py:141
  (202 shorter events, 207.6 us)
Async XLA Ops:
  0.6 326.3 %copy-start = (bf16[1024,256]{1,0:T(8,128)(2,1)S(1)}, bf16[1024,256]{1,0:T(8,128)(2,1)}, u32[]{:S(2)}) copy-start(bf16[1024,256]{1,0:T(8,128)(2,1)} %param.25) | copy-start | bytes 1572868
  0.7 5.5 %copy-start.6 = (f32[1,1024]{1,0:T(1,128)S(1)}, f32[1,1024]{1,0:T(1,128)}, u32[]{:S(2)}) copy-start(f32[1,1024]{1,0:T(1,128)} %param.18) | copy-start | bytes 12292
  0.7 5.5 %copy-start.7 = (f32[1,1024]{1,0:T(1,128)S(1)}, f32[1,1024]{1,0:T(1,128)}, u32[]{:S(2)}) copy-start(f32[1,1024]{1,0:T(1,128)} %param.21) | copy-start | bytes 12292
  6.2 320.7 %copy-start.8 = (f32[1024]{0:T(1024)S(1)}, f32[1024]{0:T(1024)}, u32[]{:S(2)}) copy-start(f32[1024]{0:T(1024)} %param.24) | copy-start | bytes 12292
  6.2 378.9 %copy-start.2 = (bf16[1024,256]{1,0:T(8,128)(2,1)S(1)}, bf16[1024,256]{1,0:T(8,128)(2,1)}, u32[]{:S(2)}) copy-start(bf16[1024,256]{1,0:T(8,128)(2,1)} %param.27) | copy-start | bytes 1572868
  6.2 378.9 %copy-start.5 = (s32[64]{0:T(128)S(1)}, s32[64]{0:T(128)}, u32[]{:S(2)}) copy-start(s32[64]{0:T(128)} %param.28) | copy-start | bytes 772
  29.5 2.7 collective-permute-start
  55.3 3.7 collective-permute-start
  70.9 1.6 copy-start.1
  82.2 6.8 %collective-permute-start = (bf16[1,197,1024]{2,1,0:T(8,128)(2,1)S(1)}, bf16[1,197,1024]{2,1,0:T(8,128)(2,1)S(1)}, u32[]{:S(2)}, u32[]{:S(2)}) collective-permute-start(bf16[1,197,1024]{2,1,0:T(8,128)(2,1)S(1)} %get-tuple-element.476), channel_id=1, source_target_pairs={{0,1},{1,2},{2,3},{4,5},{5,6},{6,7},{8,9},{9,10},{10,11},{12,13},{... | collective-permute-start | bytes 1210376 | tf_op jit(solution)/shard_map/while/body/eval_jaxpr/ppermute | solution.py:17
  112.2 9.3 %collective-permute-start = (bf16[1,197,1024]{2,1,0:T(8,128)(2,1)S(1)}, bf16[1,197,1024]{2,1,0:T(8,128)(2,1)S(1)}, u32[]{:S(2)}, u32[]{:S(2)}) collective-permute-start(bf16[1,197,1024]{2,1,0:T(8,128)(2,1)S(1)} %get-tuple-element.476), channel_id=1, source_target_pairs={{0,1},{1,2},{2,3},{4,5},{5,6},{6,7},{8,9},{9,10},{10,11},{12,13},{... | collective-permute-start | bytes 1210376 | tf_op jit(solution)/shard_map/while/body/eval_jaxpr/ppermute | solution.py:17
  133.3 1.6 copy-start.1
  144.6 9.3 %collective-permute-start = (bf16[1,197,1024]{2,1,0:T(8,128)(2,1)S(1)}, bf16[1,197,1024]{2,1,0:T(8,128)(2,1)S(1)}, u32[]{:S(2)}, u32[]{:S(2)}) collective-permute-start(bf16[1,197,1024]{2,1,0:T(8,128)(2,1)S(1)} %get-tuple-element.476), channel_id=1, source_target_pairs={{0,1},{1,2},{2,3},{4,5},{5,6},{6,7},{8,9},{9,10},{10,11},{12,13},{... | collective-permute-start | bytes 1210376 | tf_op jit(solution)/shard_map/while/body/eval_jaxpr/ppermute | solution.py:17
  165.8 1.6 copy-start.1
  177.1 9.3 %collective-permute-start = (bf16[1,197,1024]{2,1,0:T(8,128)(2,1)S(1)}, bf16[1,197,1024]{2,1,0:T(8,128)(2,1)S(1)}, u32[]{:S(2)}, u32[]{:S(2)}) collective-permute-start(bf16[1,197,1024]{2,1,0:T(8,128)(2,1)S(1)} %get-tuple-element.476), channel_id=1, source_target_pairs={{0,1},{1,2},{2,3},{4,5},{5,6},{6,7},{8,9},{9,10},{10,11},{12,13},{... | collective-permute-start | bytes 1210376 | tf_op jit(solution)/shard_map/while/body/eval_jaxpr/ppermute | solution.py:17
  198.2 1.6 copy-start.1
  209.5 9.3 %collective-permute-start = (bf16[1,197,1024]{2,1,0:T(8,128)(2,1)S(1)}, bf16[1,197,1024]{2,1,0:T(8,128)(2,1)S(1)}, u32[]{:S(2)}, u32[]{:S(2)}) collective-permute-start(bf16[1,197,1024]{2,1,0:T(8,128)(2,1)S(1)} %get-tuple-element.476), channel_id=1, source_target_pairs={{0,1},{1,2},{2,3},{4,5},{5,6},{6,7},{8,9},{9,10},{10,11},{12,13},{... | collective-permute-start | bytes 1210376 | tf_op jit(solution)/shard_map/while/body/eval_jaxpr/ppermute | solution.py:17
  230.7 1.6 copy-start.1
  242.0 9.3 %collective-permute-start = (bf16[1,197,1024]{2,1,0:T(8,128)(2,1)S(1)}, bf16[1,197,1024]{2,1,0:T(8,128)(2,1)S(1)}, u32[]{:S(2)}, u32[]{:S(2)}) collective-permute-start(bf16[1,197,1024]{2,1,0:T(8,128)(2,1)S(1)} %get-tuple-element.476), channel_id=1, source_target_pairs={{0,1},{1,2},{2,3},{4,5},{5,6},{6,7},{8,9},{9,10},{10,11},{12,13},{... | collective-permute-start | bytes 1210376 | tf_op jit(solution)/shard_map/while/body/eval_jaxpr/ppermute | solution.py:17
  252.3 31.4 %collective-permute-start = (bf16[1,197,1024]{2,1,0:T(8,128)(2,1)S(1)}, bf16[1,197,1024]{2,1,0:T(8,128)(2,1)S(1)}, u32[]{:S(2)}, u32[]{:S(2)}) collective-permute-start(bf16[1,197,1024]{2,1,0:T(8,128)(2,1)S(1)} %get-tuple-element.476), channel_id=1, source_target_pairs={{0,1},{1,2},{2,3},{4,5},{5,6},{6,7},{8,9},{9,10},{10,11},{12,13},{... | collective-permute-start | bytes 1210376 | tf_op jit(solution)/shard_map/while/body/eval_jaxpr/ppermute | solution.py:17
  284.8 9.3 %collective-permute-start = (bf16[1,197,1024]{2,1,0:T(8,128)(2,1)S(1)}, bf16[1,197,1024]{2,1,0:T(8,128)(2,1)S(1)}, u32[]{:S(2)}, u32[]{:S(2)}) collective-permute-start(bf16[1,197,1024]{2,1,0:T(8,128)(2,1)S(1)} %get-tuple-element.476), channel_id=1, source_target_pairs={{0,1},{1,2},{2,3},{4,5},{5,6},{6,7},{8,9},{9,10},{10,11},{12,13},{... | collective-permute-start | bytes 1210376 | tf_op jit(solution)/shard_map/while/body/eval_jaxpr/ppermute | solution.py:17
  295.1 31.4 %collective-permute-start = (bf16[1,197,1024]{2,1,0:T(8,128)(2,1)S(1)}, bf16[1,197,1024]{2,1,0:T(8,128)(2,1)S(1)}, u32[]{:S(2)}, u32[]{:S(2)}) collective-permute-start(bf16[1,197,1024]{2,1,0:T(8,128)(2,1)S(1)} %get-tuple-element.476), channel_id=1, source_target_pairs={{0,1},{1,2},{2,3},{4,5},{5,6},{6,7},{8,9},{9,10},{10,11},{12,13},{... | collective-permute-start | bytes 1210376 | tf_op jit(solution)/shard_map/while/body/eval_jaxpr/ppermute | solution.py:17
  326.5 59.9 %copy-start.4 = (bf16[8,256]{1,0:T(8,128)(2,1)S(1)}, bf16[8,256]{1,0:T(8,128)(2,1)}, u32[]{:S(2)}) copy-start(bf16[8,256]{1,0:T(8,128)(2,1)} %param.26) | copy-start | bytes 12292
  351.8 169.6 %copy-start.3 = (bf16[8,256]{1,0:T(8,128)(2,1)}, bf16[8,256]{1,0:T(8,128)(2,1)S(1)}, u32[]{:S(2)}) copy-start(bf16[8,256]{1,0:T(8,128)(2,1)S(1)} %psum.21) | copy-start | bytes 12292
  (3 other events, 4.8 us)
where the time goes:
time: 524 us; the launch traced here: 523 us
  blocking collectives  190 us (36%)
  matrix products  130 us (25%)
  starting transfers between devices  117 us (22%)
  other arithmetic  40.6 us (8%)
  local copies, waits for them, and re-layouts  27.6 us (5%)
  waiting for transfers between devices  14.3 us (3%)
    ppermute x11, starting transfers between devices, from_behind(): lax.ppermute(value, axis, [(source, source + steps) for source in range(i...  117 us
    dot_general x8, matrix products, encoder_block(): jnp.dot(inner, second_weight, preferred_element_type=jnp.float32)  70 us
    dot_general x8, matrix products, encoder_block(): jnp.dot(normed, qkv_weight, preferred_element_type=jnp.float32)  43.2 us
    psum x1, blocking collectives, on_device(): lax.psum(jnp.sum(jnp.exp(similarity_matrix - top[:, None]), axis=1), ('dp...  41.6 us
    pmax x1, blocking collectives, on_device(): top = lax.pmax(local_peak, ('dp', 'section'))  38.5 us
    all_gather x1, blocking collectives, on_device(): every_key = lax.all_gather(momentum_embeddings, 'dp', axis=0, tiled=True)  32.6 us
    all_gather x1, blocking collectives, on_device(): lax.all_gather(online_embeddings, 'dp', axis=0, tiled=True)  30.6 us
    psum x1, blocking collectives, broadcast(): return lax.psum(kept, axis)  24.5 us
  transfers between devices with their start and end apart: 11, of which 11 were waited for; matrix products, arithmetic and copies ran while one was open for 0% of the time, Pallas kernels for 0%

commit v1 on v0

--- a/solution.py
+++ b/solution.py
@@ -9,6 +9,24 @@
 TOKS = 197
 IMG_MB = 2
 contrastive_sharpness = 0.2
+
+
+def ring_apply(array, axis, dim, apply, out_dim):
+    size, position, extent = (lax.axis_size(axis), lax.axis_index(axis), array.shape[dim])
+    forward = [(i, (i + 1) % size) for i in range(size)]
+    held, out = (array, None)
+    for step in range(size):
+        source = (position - step) % size
+        coming = lax.ppermute(held, axis, forward) if step < size - 1 else None
+        made = apply(held, source * extent)
+        length = made.shape[out_dim]
+        if out is None:
+            out = jnp.zeros(
+                (*made.shape[:out_dim], size * length, *made.shape[out_dim + 1 :]), made.dtype
+            )
+        out = lax.dynamic_update_slice_in_dim(out, made, source * length, axis=out_dim)
+        held = coming
+    return out
 
 
 def from_behind(value, axis, steps):
@@ -115,10 +133,17 @@
     passed, finished = lax.fori_loop(0, blocks + sections - 1, advance, start)
     resident_embeddings = key_head(finished.reshape(group_images, width), final_norm_gain, w_head)
     momentum_embeddings = broadcast(resident_embeddings, "section", sections - 1)
-    query_rows_full = lax.all_gather(online_embeddings, "dp", axis=0, tiled=True)
     share = queue.shape[0]
     similarity_matrix = (
-        jnp.einsum("tw,fw->tf", query_rows_full, queue, preferred_element_type=jnp.float32)
+        ring_apply(
+            online_embeddings,
+            "dp",
+            0,
+            lambda part, at: jnp.einsum(
+                "tw,fw->tf", part, queue, preferred_element_type=jnp.float32
+            ),
+            0,
+        )
         / contrastive_sharpness
     )
     local_peak = jnp.max(similarity_matrix, axis=1)

time: 524 us -> 531 us (1.013)
  waiting for transfers between devices: 14.3 us -> 50.6 us
  blocking collectives: 190 us -> 155 us
    ppermute x0 -> x7, waiting for transfers between devices: none -> 36.3 us  [ring_apply(): coming = lax.ppermute(held, axis, forward) if step < size - 1 else None]
    all_gather x1 -> x0, blocking collectives: 30.6 us -> none  [on_device(): lax.all_gather(online_embeddings, 'dp', axis=0, tiled=True)]
  transfers between devices with their start and end apart: 11 -> 18, of which waited for: 11 -> 17; matrix products, arithmetic and copies ran while one was open for 0% -> 36% of each run, Pallas kernels for 0% -> 0%
where the time goes in v1:
time: 531 us; the launch traced here: 529 us
  blocking collectives  155 us (29%)
  matrix products  131 us (25%)
  starting transfers between devices  120 us (23%)
  waiting for transfers between devices  50.6 us (10%)
  other arithmetic  40.7 us (8%)
  local copies, waits for them, and re-layouts  27.6 us (5%)
    ppermute x11, starting transfers between devices, from_behind(): lax.ppermute(value, axis, [(source, source + steps) for source in range(i...  117 us
    dot_general x8, matrix products, encoder_block(): jnp.dot(inner, second_weight, preferred_element_type=jnp.float32)  70 us
    dot_general x8, matrix products, encoder_block(): jnp.dot(normed, qkv_weight, preferred_element_type=jnp.float32)  43.2 us
    psum x1, blocking collectives, on_device(): lax.psum(jnp.sum(jnp.exp(similarity_matrix - top[:, None]), axis=1), ('dp...  41.2 us
    pmax x1, blocking collectives, on_device(): top = lax.pmax(local_peak, ('dp', 'section'))  36.9 us
    ppermute x7, waiting for transfers between devices, ring_apply(): coming = lax.ppermute(held, axis, forward) if step < size - 1 else None  36.3 us
    all_gather x1, blocking collectives, on_device(): every_key = lax.all_gather(momentum_embeddings, 'dp', axis=0, tiled=True)  31.1 us
    psum x1, blocking collectives, broadcast(): return lax.psum(kept, axis)  24.5 us
  transfers between devices with their start and end apart: 18, of which 17 were waited for; matrix products, arithmetic and copies ran while one was open for 36% of the time, Pallas kernels for 0%

profile of v1, /device:TPU:0, one launch (start us, length us, event | category | flops | bytes accessed | tf_op | source)
XLA Modules:
  0.0 528.8 jit_solution(15056592170406225824)
XLA Ops:
  9.2 320.3 %while.17 = (s32[]{:T(128)}, bf16[1,197,1024]{2,1,0:T(8,128)(2,1)S(1)}, bf16[8,1,1024]{2,1,0:T(2,128)(2,1)S(1)}, s32[]{:T(128)}, pred[]{:T(512)}, /*index=5*/bf1...) while((s32[]{:T(128)}, ...), condition=%wide.region_9.10_spmd, body=%wide.region_0.9_spmd.sunk | while | flops 3499673600 | bytes 49231128 | solution.py:133
  10.4 22.1 %conditional.2 = (bf16[1,197,1024]{2,1,0:T(8,128)(2,1)S(1)}) conditional(s32[]{:T(128)} %convert_element_type.128, bf16[1,197,1024]{2,1,0:T(8,128)(2,1)S(1)} %bitcast_select_fusion.2, (bf16[1,197,1024]{2,1,0:T(8,128)(2,1)S(1)}, f32[1,1024]{1,0:T(1,128)S(1)}, bf16[1,1024,3072]{2,1,0:T(8,128)(2,1)}, bf16[1,1024,1024]{2,1,0:T(8,128)(2,1)}, ...), branch_computations={%region_1.1_spmd, %region_2.8_spmd} | conditional | flops 3499470848 | bytes 46394252 | solution.py:125
  23.7 8.7 %fusion.40 = bf16[1,197,1024]{2,1,0:T(8,128)(2,1)S(1)} fusion(f32[1,197,1024]{2,1,0:T(8,128)S(1)} %get-tuple-element.344, bf16[1,2048,1024]{2,1,0:T(8,128)(2,1)} %get-tuple-element.295, bf16[1,1024,2048]{2,1,0:T(8,128)(2,1)} %get-tuple-element.294, f32[1024]{0:T(1024)S(1)} %bitcast.107, f32[197]{0:T(256)S(1)} %add_rsqrt_fusion, ...), kind=kOutput, calls=%fused_computation.40 | convolution fusion | flops 1679990784 | bytes 9604648 | tf_op jit(solution)/shard_map/while/body/eval_jaxpr/cond/branch_1_fun/dot_general | solution.py:75
  36.2 22.1 %conditional.2 = (bf16[1,197,1024]{2,1,0:T(8,128)(2,1)S(1)}) conditional(s32[]{:T(128)} %convert_element_type.128, bf16[1,197,1024]{2,1,0:T(8,128)(2,1)S(1)} %bitcast_select_fusion.2, (bf16[1,197,1024]{2,1,0:T(8,128)(2,1)S(1)}, f32[1,1024]{1,0:T(1,128)S(1)}, bf16[1,1024,3072]{2,1,0:T(8,128)(2,1)}, bf16[1,1024,1024]{2,1,0:T(8,128)(2,1)}, ...), branch_computations={%region_1.1_spmd, %region_2.8_spmd} | conditional | flops 3499470848 | bytes 46394252 | solution.py:125
  49.6 8.7 %fusion.40 = bf16[1,197,1024]{2,1,0:T(8,128)(2,1)S(1)} fusion(f32[1,197,1024]{2,1,0:T(8,128)S(1)} %get-tuple-element.344, bf16[1,2048,1024]{2,1,0:T(8,128)(2,1)} %get-tuple-element.295, bf16[1,1024,2048]{2,1,0:T(8,128)(2,1)} %get-tuple-element.294, f32[1024]{0:T(1024)S(1)} %bitcast.107, f32[197]{0:T(256)S(1)} %add_rsqrt_fusion, ...), kind=kOutput, calls=%fused_computation.40 | convolution fusion | flops 1679990784 | bytes 9604648 | tf_op jit(solution)/shard_map/while/body/eval_jaxpr/cond/branch_1_fun/dot_general | solution.py:75
  63.0 22.1 %conditional.2 = (bf16[1,197,1024]{2,1,0:T(8,128)(2,1)S(1)}) conditional(s32[]{:T(128)} %convert_element_type.128, bf16[1,197,1024]{2,1,0:T(8,128)(2,1)S(1)} %bitcast_select_fusion.2, (bf16[1,197,1024]{2,1,0:T(8,128)(2,1)S(1)}, f32[1,1024]{1,0:T(1,128)S(1)}, bf16[1,1024,3072]{2,1,0:T(8,128)(2,1)}, bf16[1,1024,1024]{2,1,0:T(8,128)(2,1)}, ...), branch_computations={%region_1.1_spmd, %region_2.8_spmd} | conditional | flops 3499470848 | bytes 46394252 | solution.py:125
  76.4 8.7 %fusion.40 = bf16[1,197,1024]{2,1,0:T(8,128)(2,1)S(1)} fusion(f32[1,197,1024]{2,1,0:T(8,128)S(1)} %get-tuple-element.344, bf16[1,2048,1024]{2,1,0:T(8,128)(2,1)} %get-tuple-element.295, bf16[1,1024,2048]{2,1,0:T(8,128)(2,1)} %get-tuple-element.294, f32[1024]{0:T(1024)S(1)} %bitcast.107, f32[197]{0:T(256)S(1)} %add_rsqrt_fusion, ...), kind=kOutput, calls=%fused_computation.40 | convolution fusion | flops 1679990784 | bytes 9604648 | tf_op jit(solution)/shard_map/while/body/eval_jaxpr/cond/branch_1_fun/dot_general | solution.py:75
  93.0 22.1 %conditional.2 = (bf16[1,197,1024]{2,1,0:T(8,128)(2,1)S(1)}) conditional(s32[]{:T(128)} %convert_element_type.128, bf16[1,197,1024]{2,1,0:T(8,128)(2,1)S(1)} %bitcast_select_fusion.2, (bf16[1,197,1024]{2,1,0:T(8,128)(2,1)S(1)}, f32[1,1024]{1,0:T(1,128)S(1)}, bf16[1,1024,3072]{2,1,0:T(8,128)(2,1)}, bf16[1,1024,1024]{2,1,0:T(8,128)(2,1)}, ...), branch_computations={%region_1.1_spmd, %region_2.8_spmd} | conditional | flops 3499470848 | bytes 46394252 | solution.py:125
  106.4 8.7 %fusion.40 = bf16[1,197,1024]{2,1,0:T(8,128)(2,1)S(1)} fusion(f32[1,197,1024]{2,1,0:T(8,128)S(1)} %get-tuple-element.344, bf16[1,2048,1024]{2,1,0:T(8,128)(2,1)} %get-tuple-element.295, bf16[1,1024,2048]{2,1,0:T(8,128)(2,1)} %get-tuple-element.294, f32[1024]{0:T(1024)S(1)} %bitcast.107, f32[197]{0:T(256)S(1)} %add_rsqrt_fusion, ...), kind=kOutput, calls=%fused_computation.40 | convolution fusion | flops 1679990784 | bytes 9604648 | tf_op jit(solution)/shard_map/while/body/eval_jaxpr/cond/branch_1_fun/dot_general | solution.py:75
  125.5 22.1 %conditional.2 = (bf16[1,197,1024]{2,1,0:T(8,128)(2,1)S(1)}) conditional(s32[]{:T(128)} %convert_element_type.128, bf16[1,197,1024]{2,1,0:T(8,128)(2,1)S(1)} %bitcast_select_fusion.2, (bf16[1,197,1024]{2,1,0:T(8,128)(2,1)S(1)}, f32[1,1024]{1,0:T(1,128)S(1)}, bf16[1,1024,3072]{2,1,0:T(8,128)(2,1)}, bf16[1,1024,1024]{2,1,0:T(8,128)(2,1)}, ...), branch_computations={%region_1.1_spmd, %region_2.8_spmd} | conditional | flops 3499470848 | bytes 46394252 | solution.py:125
  138.9 8.7 %fusion.40 = bf16[1,197,1024]{2,1,0:T(8,128)(2,1)S(1)} fusion(f32[1,197,1024]{2,1,0:T(8,128)S(1)} %get-tuple-element.344, bf16[1,2048,1024]{2,1,0:T(8,128)(2,1)} %get-tuple-element.295, bf16[1,1024,2048]{2,1,0:T(8,128)(2,1)} %get-tuple-element.294, f32[1024]{0:T(1024)S(1)} %bitcast.107, f32[197]{0:T(256)S(1)} %add_rsqrt_fusion, ...), kind=kOutput, calls=%fused_computation.40 | convolution fusion | flops 1679990784 | bytes 9604648 | tf_op jit(solution)/shard_map/while/body/eval_jaxpr/cond/branch_1_fun/dot_general | solution.py:75
  157.9 22.1 %conditional.2 = (bf16[1,197,1024]{2,1,0:T(8,128)(2,1)S(1)}) conditional(s32[]{:T(128)} %convert_element_type.128, bf16[1,197,1024]{2,1,0:T(8,128)(2,1)S(1)} %bitcast_select_fusion.2, (bf16[1,197,1024]{2,1,0:T(8,128)(2,1)S(1)}, f32[1,1024]{1,0:T(1,128)S(1)}, bf16[1,1024,3072]{2,1,0:T(8,128)(2,1)}, bf16[1,1024,1024]{2,1,0:T(8,128)(2,1)}, ...), branch_computations={%region_1.1_spmd, %region_2.8_spmd} | conditional | flops 3499470848 | bytes 46394252 | solution.py:125
  171.3 8.7 %fusion.40 = bf16[1,197,1024]{2,1,0:T(8,128)(2,1)S(1)} fusion(f32[1,197,1024]{2,1,0:T(8,128)S(1)} %get-tuple-element.344, bf16[1,2048,1024]{2,1,0:T(8,128)(2,1)} %get-tuple-element.295, bf16[1,1024,2048]{2,1,0:T(8,128)(2,1)} %get-tuple-element.294, f32[1024]{0:T(1024)S(1)} %bitcast.107, f32[197]{0:T(256)S(1)} %add_rsqrt_fusion, ...), kind=kOutput, calls=%fused_computation.40 | convolution fusion | flops 1679990784 | bytes 9604648 | tf_op jit(solution)/shard_map/while/body/eval_jaxpr/cond/branch_1_fun/dot_general | solution.py:75
  190.4 22.1 %conditional.2 = (bf16[1,197,1024]{2,1,0:T(8,128)(2,1)S(1)}) conditional(s32[]{:T(128)} %convert_element_type.128, bf16[1,197,1024]{2,1,0:T(8,128)(2,1)S(1)} %bitcast_select_fusion.2, (bf16[1,197,1024]{2,1,0:T(8,128)(2,1)S(1)}, f32[1,1024]{1,0:T(1,128)S(1)}, bf16[1,1024,3072]{2,1,0:T(8,128)(2,1)}, bf16[1,1024,1024]{2,1,0:T(8,128)(2,1)}, ...), branch_computations={%region_1.1_spmd, %region_2.8_spmd} | conditional | flops 3499470848 | bytes 46394252 | solution.py:125
  203.8 8.7 %fusion.40 = bf16[1,197,1024]{2,1,0:T(8,128)(2,1)S(1)} fusion(f32[1,197,1024]{2,1,0:T(8,128)S(1)} %get-tuple-element.344, bf16[1,2048,1024]{2,1,0:T(8,128)(2,1)} %get-tuple-element.295, bf16[1,1024,2048]{2,1,0:T(8,128)(2,1)} %get-tuple-element.294, f32[1024]{0:T(1024)S(1)} %bitcast.107, f32[197]{0:T(256)S(1)} %add_rsqrt_fusion, ...), kind=kOutput, calls=%fused_computation.40 | convolution fusion | flops 1679990784 | bytes 9604648 | tf_op jit(solution)/shard_map/while/body/eval_jaxpr/cond/branch_1_fun/dot_general | solution.py:75
  222.8 22.1 %conditional.2 = (bf16[1,197,1024]{2,1,0:T(8,128)(2,1)S(1)}) conditional(s32[]{:T(128)} %convert_element_type.128, bf16[1,197,1024]{2,1,0:T(8,128)(2,1)S(1)} %bitcast_select_fusion.2, (bf16[1,197,1024]{2,1,0:T(8,128)(2,1)S(1)}, f32[1,1024]{1,0:T(1,128)S(1)}, bf16[1,1024,3072]{2,1,0:T(8,128)(2,1)}, bf16[1,1024,1024]{2,1,0:T(8,128)(2,1)}, ...), branch_computations={%region_1.1_spmd, %region_2.8_spmd} | conditional | flops 3499470848 | bytes 46394252 | solution.py:125
  236.2 8.7 %fusion.40 = bf16[1,197,1024]{2,1,0:T(8,128)(2,1)S(1)} fusion(f32[1,197,1024]{2,1,0:T(8,128)S(1)} %get-tuple-element.344, bf16[1,2048,1024]{2,1,0:T(8,128)(2,1)} %get-tuple-element.295, bf16[1,1024,2048]{2,1,0:T(8,128)(2,1)} %get-tuple-element.294, f32[1024]{0:T(1024)S(1)} %bitcast.107, f32[197]{0:T(256)S(1)} %add_rsqrt_fusion, ...), kind=kOutput, calls=%fused_computation.40 | convolution fusion | flops 1679990784 | bytes 9604648 | tf_op jit(solution)/shard_map/while/body/eval_jaxpr/cond/branch_1_fun/dot_general | solution.py:75
  255.3 30.1 %collective-permute-start = (bf16[1,197,1024]{2,1,0:T(8,128)(2,1)S(1)}, bf16[1,197,1024]{2,1,0:T(8,128)(2,1)S(1)}, u32[]{:S(2)}, u32[]{:S(2)}) collective-permute-start(bf16[1,197,1024]{2,1,0:T(8,128)(2,1)S(1)} %get-tuple-element.474), channel_id=1, source_target_pairs={{0,1},{1,2},{2,3},{4,5},{5,6},{6,7},{8,9},{9,10},{10,11},{12,13},{... | collective-permute-start | bytes 1210376 | tf_op jit(solution)/shard_map/while/body/eval_jaxpr/ppermute | solution.py:35
  298.1 30.1 %collective-permute-start = (bf16[1,197,1024]{2,1,0:T(8,128)(2,1)S(1)}, bf16[1,197,1024]{2,1,0:T(8,128)(2,1)S(1)}, u32[]{:S(2)}, u32[]{:S(2)}) collective-permute-start(bf16[1,197,1024]{2,1,0:T(8,128)(2,1)S(1)} %get-tuple-element.474), channel_id=1, source_target_pairs={{0,1},{1,2},{2,3},{4,5},{5,6},{6,7},{8,9},{9,10},{10,11},{12,13},{... | collective-permute-start | bytes 1210376 | tf_op jit(solution)/shard_map/while/body/eval_jaxpr/ppermute | solution.py:35
  330.3 24.5 %psum.21 = bf16[8,256]{1,0:T(8,128)(2,1)S(1)} all-reduce(bf16[8,256]{1,0:T(8,128)(2,1)S(1)} %fusion.136), channel_id=1, replica_groups=mesh['dp'=8,'section'=4] {'section'}, use_global_device_ids=true, to_apply=%region_13.14 | all-reduce | flops 2048 | bytes 8192 | tf_op jit(solution)/shard_map/psum | solution.py:40
  355.0 31.1 %all_gather.3 = bf16[64,256]{1,0:T(8,128)(2,1)S(1)} all-gather(bf16[8,256]{1,0:T(8,128)(2,1)S(1)} %psum.21), channel_id=1, replica_groups=mesh['dp'=8,'section'=4] {'dp'}, dimensions={0}, use_global_device_ids=true | all-gather | bytes 36864 | tf_op jit(solution)/shard_map/all_gather | solution.py:168
  426.5 36.9 %pmax.7 = f32[64]{0:T(128)S(1)} all-reduce(f32[64]{0:T(128)S(1)} %multiply_reduce_fusion.2), channel_id=1, replica_groups=mesh['dp'=8,'section'=4] {'dp','section'}, use_global_device_ids=true, to_apply=%region_15.16 | all-reduce | flops 64 | bytes 512 | tf_op jit(solution)/shard_map/pmax | solution.py:150
  463.6 41.2 %psum.22 = f32[64]{0:T(128)S(1)} all-reduce(f32[64]{0:T(128)S(1)} %exponential_reduce_fusion), channel_id=1, replica_groups=mesh['dp'=8,'section'=4] {'dp','section'}, use_global_device_ids=true, to_apply=%region_17.18 | all-reduce | flops 64 | bytes 512 | tf_op jit(solution)/shard_map/psum | solution.py:151
  506.0 21.0 %psum.23 = f32[]{:T(128)} all-reduce(f32[]{:T(128)} %get-tuple-element.339), channel_id=1, replica_groups=mesh['dp'=8,'section'=4] {'dp'}, use_global_device_ids=true, to_apply=%region_20.21 | all-reduce | flops 1 | bytes 8 | tf_op jit(solution)/shard_map/psum | solution.py:166
  (224 shorter events, 239.9 us)
Async XLA Ops:
  0.6 329.3 %copy-start = (bf16[1024,256]{1,0:T(8,128)(2,1)S(1)}, bf16[1024,256]{1,0:T(8,128)(2,1)}, u32[]{:S(2)}) copy-start(bf16[1024,256]{1,0:T(8,128)(2,1)} %param.25) | copy-start | bytes 1572868
  0.6 387.7 %collective-permute-start.1 = (bf16[8,256]{1,0:T(8,128)(2,1)}, bf16[8,256]{1,0:T(8,128)(2,1)S(1)}, u32[]{:S(2)}, u32[]{:S(2)}) collective-permute-start(bf16[8,256]{1,0:T(8,128)(2,1)} %param.26), channel_id=1, source_target_pairs={{0,4},{4,8},{8,12},{12,16},{16,20},{20,24},{24,28},{28,0},{1,5},{5... | collective-permute-start | bytes 12296 | tf_op jit(solution)/shard_map/ppermute | solution.py:20
  9.2 320.7 %copy-start.8 = (f32[1024]{0:T(1024)S(1)}, f32[1024]{0:T(1024)}, u32[]{:S(2)}) copy-start(f32[1024]{0:T(1024)} %param.24) | copy-start | bytes 12292
  9.2 345.6 %copy-start.4 = (bf16[8,256]{1,0:T(8,128)(2,1)S(1)}, bf16[8,256]{1,0:T(8,128)(2,1)}, u32[]{:S(2)}) copy-start(bf16[8,256]{1,0:T(8,128)(2,1)} %param.26) | copy-start | bytes 12292
  9.2 377.6 %copy-start.2 = (bf16[1024,256]{1,0:T(8,128)(2,1)S(1)}, bf16[1024,256]{1,0:T(8,128)(2,1)}, u32[]{:S(2)}) copy-start(bf16[1024,256]{1,0:T(8,128)(2,1)} %param.27) | copy-start | bytes 1572868
  32.5 2.7 collective-permute-start
  58.3 3.7 collective-permute-start
  85.2 6.8 %collective-permute-start = (bf16[1,197,1024]{2,1,0:T(8,128)(2,1)S(1)}, bf16[1,197,1024]{2,1,0:T(8,128)(2,1)S(1)}, u32[]{:S(2)}, u32[]{:S(2)}) collective-permute-start(bf16[1,197,1024]{2,1,0:T(8,128)(2,1)S(1)} %get-tuple-element.474), channel_id=1, source_target_pairs={{0,1},{1,2},{2,3},{4,5},{5,6},{6,7},{8,9},{9,10},{10,11},{12,13},{... | collective-permute-start | bytes 1210376 | tf_op jit(solution)/shard_map/while/body/eval_jaxpr/ppermute | solution.py:35
  115.2 9.3 %collective-permute-start = (bf16[1,197,1024]{2,1,0:T(8,128)(2,1)S(1)}, bf16[1,197,1024]{2,1,0:T(8,128)(2,1)S(1)}, u32[]{:S(2)}, u32[]{:S(2)}) collective-permute-start(bf16[1,197,1024]{2,1,0:T(8,128)(2,1)S(1)} %get-tuple-element.474), channel_id=1, source_target_pairs={{0,1},{1,2},{2,3},{4,5},{5,6},{6,7},{8,9},{9,10},{10,11},{12,13},{... | collective-permute-start | bytes 1210376 | tf_op jit(solution)/shard_map/while/body/eval_jaxpr/ppermute | solution.py:35
  147.6 9.3 %collective-permute-start = (bf16[1,197,1024]{2,1,0:T(8,128)(2,1)S(1)}, bf16[1,197,1024]{2,1,0:T(8,128)(2,1)S(1)}, u32[]{:S(2)}, u32[]{:S(2)}) collective-permute-start(bf16[1,197,1024]{2,1,0:T(8,128)(2,1)S(1)} %get-tuple-element.474), channel_id=1, source_target_pairs={{0,1},{1,2},{2,3},{4,5},{5,6},{6,7},{8,9},{9,10},{10,11},{12,13},{... | collective-permute-start | bytes 1210376 | tf_op jit(solution)/shard_map/while/body/eval_jaxpr/ppermute | solution.py:35
  180.1 9.3 %collective-permute-start = (bf16[1,197,1024]{2,1,0:T(8,128)(2,1)S(1)}, bf16[1,197,1024]{2,1,0:T(8,128)(2,1)S(1)}, u32[]{:S(2)}, u32[]{:S(2)}) collective-permute-start(bf16[1,197,1024]{2,1,0:T(8,128)(2,1)S(1)} %get-tuple-element.474), channel_id=1, source_target_pairs={{0,1},{1,2},{2,3},{4,5},{5,6},{6,7},{8,9},{9,10},{10,11},{12,13},{... | collective-permute-start | bytes 1210376 | tf_op jit(solution)/shard_map/while/body/eval_jaxpr/ppermute | solution.py:35
  212.5 9.3 %collective-permute-start = (bf16[1,197,1024]{2,1,0:T(8,128)(2,1)S(1)}, bf16[1,197,1024]{2,1,0:T(8,128)(2,1)S(1)}, u32[]{:S(2)}, u32[]{:S(2)}) collective-permute-start(bf16[1,197,1024]{2,1,0:T(8,128)(2,1)S(1)} %get-tuple-element.474), channel_id=1, source_target_pairs={{0,1},{1,2},{2,3},{4,5},{5,6},{6,7},{8,9},{9,10},{10,11},{12,13},{... | collective-permute-start | bytes 1210376 | tf_op jit(solution)/shard_map/while/body/eval_jaxpr/ppermute | solution.py:35
  245.0 9.3 %collective-permute-start = (bf16[1,197,1024]{2,1,0:T(8,128)(2,1)S(1)}, bf16[1,197,1024]{2,1,0:T(8,128)(2,1)S(1)}, u32[]{:S(2)}, u32[]{:S(2)}) collective-permute-start(bf16[1,197,1024]{2,1,0:T(8,128)(2,1)S(1)} %get-tuple-element.474), channel_id=1, source_target_pairs={{0,1},{1,2},{2,3},{4,5},{5,6},{6,7},{8,9},{9,10},{10,11},{12,13},{... | collective-permute-start | bytes 1210376 | tf_op jit(solution)/shard_map/while/body/eval_jaxpr/ppermute | solution.py:35
  255.3 31.4 %collective-permute-start = (bf16[1,197,1024]{2,1,0:T(8,128)(2,1)S(1)}, bf16[1,197,1024]{2,1,0:T(8,128)(2,1)S(1)}, u32[]{:S(2)}, u32[]{:S(2)}) collective-permute-start(bf16[1,197,1024]{2,1,0:T(8,128)(2,1)S(1)} %get-tuple-element.474), channel_id=1, source_target_pairs={{0,1},{1,2},{2,3},{4,5},{5,6},{6,7},{8,9},{9,10},{10,11},{12,13},{... | collective-permute-start | bytes 1210376 | tf_op jit(solution)/shard_map/while/body/eval_jaxpr/ppermute | solution.py:35
  287.8 9.3 %collective-permute-start = (bf16[1,197,1024]{2,1,0:T(8,128)(2,1)S(1)}, bf16[1,197,1024]{2,1,0:T(8,128)(2,1)S(1)}, u32[]{:S(2)}, u32[]{:S(2)}) collective-permute-start(bf16[1,197,1024]{2,1,0:T(8,128)(2,1)S(1)} %get-tuple-element.474), channel_id=1, source_target_pairs={{0,1},{1,2},{2,3},{4,5},{5,6},{6,7},{8,9},{9,10},{10,11},{12,13},{... | collective-permute-start | bytes 1210376 | tf_op jit(solution)/shard_map/while/body/eval_jaxpr/ppermute | solution.py:35
  298.1 31.4 %collective-permute-start = (bf16[1,197,1024]{2,1,0:T(8,128)(2,1)S(1)}, bf16[1,197,1024]{2,1,0:T(8,128)(2,1)S(1)}, u32[]{:S(2)}, u32[]{:S(2)}) collective-permute-start(bf16[1,197,1024]{2,1,0:T(8,128)(2,1)S(1)} %get-tuple-element.474), channel_id=1, source_target_pairs={{0,1},{1,2},{2,3},{4,5},{5,6},{6,7},{8,9},{9,10},{10,11},{12,13},{... | collective-permute-start | bytes 1210376 | tf_op jit(solution)/shard_map/while/body/eval_jaxpr/ppermute | solution.py:35
  329.5 57.5 %copy-start.5 = (s32[64]{0:T(128)S(1)}, s32[64]{0:T(128)}, u32[]{:S(2)}) copy-start(s32[64]{0:T(128)} %param.28) | copy-start | bytes 772
  354.8 46.4 %copy-start.3 = (bf16[8,256]{1,0:T(8,128)(2,1)}, bf16[8,256]{1,0:T(8,128)(2,1)S(1)}, u32[]{:S(2)}) copy-start(bf16[8,256]{1,0:T(8,128)(2,1)S(1)} %psum.21) | copy-start | bytes 12292
  388.3 6.3 %collective-permute-start.2 = (bf16[8,256]{1,0:T(8,128)(2,1)S(1)}, bf16[8,256]{1,0:T(8,128)(2,1)S(1)}, u32[]{:S(2)}, u32[]{:S(2)}) collective-permute-start(bf16[8,256]{1,0:T(8,128)(2,1)S(1)} %collective-permute-done.1), channel_id=1, source_target_pairs={{0,4},{4,8},{8,12},{12,16},{16,20},{20,24},{24,28},{28,0},{1,5},{5... | collective-permute-start | bytes 12296 | tf_op jit(solution)/shard_map/ppermute | solution.py:20
  394.6 6.3 %collective-permute-start.3 = (bf16[8,256]{1,0:T(8,128)(2,1)S(1)}, bf16[8,256]{1,0:T(8,128)(2,1)S(1)}, u32[]{:S(2)}, u32[]{:S(2)}) collective-permute-start(bf16[8,256]{1,0:T(8,128)(2,1)S(1)} %collective-permute-done.2), channel_id=1, source_target_pairs={{0,4},{4,8},{8,12},{12,16},{16,20},{20,24},{24,28},{28,0},{1,5},{5... | collective-permute-start | bytes 12296 | tf_op jit(solution)/shard_map/ppermute | solution.py:20
  400.9 6.3 %collective-permute-start.4 = (bf16[8,256]{1,0:T(8,128)(2,1)S(1)}, bf16[8,256]{1,0:T(8,128)(2,1)S(1)}, u32[]{:S(2)}, u32[]{:S(2)}) collective-permute-start(bf16[8,256]{1,0:T(8,128)(2,1)S(1)} %collective-permute-done.3), channel_id=1, source_target_pairs={{0,4},{4,8},{8,12},{12,16},{16,20},{20,24},{24,28},{28,0},{1,5},{5... | collective-permute-start | bytes 12296 | tf_op jit(solution)/shard_map/ppermute | solution.py:20
  407.3 6.3 %collective-permute-start.5 = (bf16[8,256]{1,0:T(8,128)(2,1)S(1)}, bf16[8,256]{1,0:T(8,128)(2,1)S(1)}, u32[]{:S(2)}, u32[]{:S(2)}) collective-permute-start(bf16[8,256]{1,0:T(8,128)(2,1)S(1)} %collective-permute-done.4), channel_id=1, source_target_pairs={{0,4},{4,8},{8,12},{12,16},{16,20},{20,24},{24,28},{28,0},{1,5},{5... | collective-permute-start | bytes 12296 | tf_op jit(solution)/shard_map/ppermute | solution.py:20
  413.6 6.3 %collective-permute-start.6 = (bf16[8,256]{1,0:T(8,128)(2,1)S(1)}, bf16[8,256]{1,0:T(8,128)(2,1)S(1)}, u32[]{:S(2)}, u32[]{:S(2)}) collective-permute-start(bf16[8,256]{1,0:T(8,128)(2,1)S(1)} %collective-permute-done.5), channel_id=1, source_target_pairs={{0,4},{4,8},{8,12},{12,16},{16,20},{20,24},{24,28},{28,0},{1,5},{5... | collective-permute-start | bytes 12296 | tf_op jit(solution)/shard_map/ppermute | solution.py:20
  419.9 6.3 %collective-permute-start.7 = (bf16[8,256]{1,0:T(8,128)(2,1)S(1)}, bf16[8,256]{1,0:T(8,128)(2,1)S(1)}, u32[]{:S(2)}, u32[]{:S(2)}) collective-permute-start(bf16[8,256]{1,0:T(8,128)(2,1)S(1)} %collective-permute-done.6), channel_id=1, source_target_pairs={{0,4},{4,8},{8,12},{12,16},{16,20},{20,24},{24,28},{28,0},{1,5},{5... | collective-permute-start | bytes 12296 | tf_op jit(solution)/shard_map/ppermute | solution.py:20
  (10 other events, 23.7 us)
